TPU v7x, 32 devices: a whole 2x2x4 slice. The times are simulated.
32 devices in a mesh: gx: 8 (over y, x, core), gy: 4 (over z).
Axes of the slice: x: 2, y: 2, z: 4, core: 2. Of those that a mesh axis runs over, the one named last changes fastest.
Arguments:
- rhs: float32 [8, 125, 512], P('gx', None, 'gy'), may hold values from -6 to 6
- inverse: bfloat16 [8, 125, 125, 512], P('gx', None, None, 'gy')
- weights: float32 [8, 4, 512], P('gx', None, 'gy'), may hold values from 0.12 to 0.3
- neighbours: int32 [8, 4, 512], P('gx', None, 'gy'), may hold values from 0 to 383, as said below
- send_lists: int32 [8, 4, 256], P('gx', None, 'gy'), may hold values from 0 to 127
- coloring: int32 [8, 4], P('gx', 'gy'), may hold values from 0 to 3, as said below
Outputs:
- solution: float32 [8, 125, 512], P('gx', None, 'gy')
- norms: float32 [2], replicated
Inputs may be any that keep to these rules, and one draw needn't show every extreme that they name: `coloring`: the color of subdomain (i, j) depends only on i mod 2 and j mod 2, and the four parity classes have four different colors; which class has which color varies. `neighbours`: slots below 128 are the subdomain's own faces, the rest the received intersection faces in the order of the steps; every received slot is used by some face.
All inputs are finite; a program needn't handle non-finite values.
Results may differ from a plain program's by a relative error of at most 0.0055.
Values sent between devices are 32-bit elements; how exact they have to be, the bound alone decides.
No kernel may reach another device: no remote copies, remote signals or barrier semaphores. Data moves between devices by JAX's collectives and lax.ppermute only.
A program may use at most 64 MiB of HBM per device.

v0:
```python
import jax
import jax.numpy as jnp
from jax import lax
from jax.experimental import pallas as pl
from jax.experimental.pallas import tpu as pltpu
from jax.sharding import PartitionSpec as P

LANES = 128
SUB = 8
GROUP = 36
VMEM_LIMIT = 16 * 1024 * 1024
CHUNKS = 5
FIRST, SECOND, CONTROL = range(3)

VSPEC = pl.BlockSpec(memory_space=pltpu.VMEM)
SSPEC = pl.BlockSpec(memory_space=pltpu.SMEM)


def vmem(value):
    return pltpu.with_memory_space_constraint(value, pltpu.VMEM)


def hbm(value):
    return pltpu.with_memory_space_constraint(value, pltpu.HBM)


def smem(value):
    return pltpu.with_memory_space_constraint(value, pltpu.SMEM)


class Plan:
    def __init__(self, mesh, rows, faces, halo, neigh):
        self.nx, self.ny = mesh.shape["gx"], mesh.shape["gy"]
        self.rows, self.faces, self.halo, self.neigh = rows, faces, halo, neigh
        assert self.nx % 2 == 0 and self.ny % 2 == 0
        assert faces == LANES and 2 * halo == LANES
        self.tiles = -(-rows // (2 * SUB)) * 2
        self.pad = self.tiles * SUB
        self.half = self.pad // 2
        self.held = rows * 18 // 25 // CHUNKS * CHUNKS
        self.along = (self.pad, 2 * self.pad)
        self.rhs = 3 * self.pad
        self.norm = 4 * self.pad
        self.step = self.norm + 2 * SUB
        self.state = self.step + SUB
        self.state_type = pltpu.VMEM((self.state, LANES), jnp.float32)
        self.pack_type = pltpu.VMEM((self.half, LANES), jnp.float32)
        self.control_type = pltpu.SMEM((CONTROL,), jnp.int32)

    def held_type(self, inverse):
        return pltpu.VMEM((self.held, *inverse.shape[1:]), inverse.dtype)

    def rest_type(self, inverse):
        return pltpu.VMEM((self.rows - self.held, *inverse.shape[1:]), inverse.dtype)


def write_pack(plan, state, lists, row, ref):
    low = lax.broadcasted_iota(jnp.int32, (SUB, LANES), 1) < plan.halo
    index = jnp.broadcast_to(lists[pl.ds(row, 1), :], (SUB, LANES))

    def take(t):
        tile = state[t * SUB:(t + 1) * SUB, :]
        return jnp.take_along_axis(tile, index, axis=1, mode="promise_in_bounds")

    for t in range(plan.tiles // 2):
        ref[t * SUB:(t + 1) * SUB, :] = jnp.where(low, take(t), take(t + plan.tiles // 2))


def merge(plan, state, base, even, odd, there):
    low = lax.broadcasted_iota(jnp.int32, (SUB, LANES), 1) < plan.halo
    for t in range(plan.tiles // 2):
        a = even[t * SUB:(t + 1) * SUB, :]
        b = jnp.where(there, odd[t * SUB:(t + 1) * SUB, :], 0.0)
        first = jnp.where(low, a, pltpu.roll(b, plan.halo, 1))
        second = jnp.where(low, pltpu.roll(a, plan.halo, 1), b)
        state[pl.ds(base + t * SUB, SUB), :] = first
        state[pl.ds(base + plan.half + t * SUB, SUB), :] = second


def apply_inverse(plan, blocks, source, result, base, start, stop):
    src = source[0:plan.rows, :]
    group = max(g for g in range(1, GROUP + 1) if (stop - start) % g == 0)

    def step(n, carry):
        for k in range(group):
            i = start + n * group + k
            block = blocks[i].astype(jnp.float32)
            result[pl.ds(base + i, 1), :] = jnp.sum(block * src, axis=0, keepdims=True)
        return carry

    lax.fori_loop(0, (stop - start) // group, step, 0)


def pieces(plan):
    chunk = plan.held // CHUNKS
    return [(n * chunk, (n + 1) * chunk) for n in range(CHUNKS)] + [(plan.held, plan.rows)]


def piece_copy(plan, n, inverse, kept, rest, sem):
    start, stop = pieces(plan)[n]
    target = kept.at[pl.ds(start, stop - start)] if n < CHUNKS else rest
    return pltpu.make_async_copy(inverse.at[pl.ds(start, stop - start)], target, sem)


def parts_of(value):
    high = value.astype(jnp.bfloat16)
    low = (value - high.astype(jnp.float32)).astype(jnp.bfloat16)
    return high, low


def update(plan, second, state, coupling, inverse, kept, rest, source, result, sem):
    again = piece_copy(plan, CHUNKS, inverse, kept, rest, sem)
    again.start()
    pad = plan.pad
    values = jnp.concatenate([state[n * pad:(n + 1) * pad, :] for n in range(3)], axis=1)
    high, low = parts_of(values)
    size = 3 * LANES
    couple = jnp.dot(high, coupling[0:size, :], preferred_element_type=jnp.float32)
    couple = couple + jnp.dot(low, coupling[0:size, :], preferred_element_type=jnp.float32)
    couple = couple + jnp.dot(high, coupling[size:2 * size, :], preferred_element_type=jnp.float32)
    right = state[plan.rhs:plan.rhs + pad, :]
    source[...] = (right + couple).astype(jnp.bfloat16).astype(jnp.float32)
    result[pad - SUB:pad, :] = jnp.zeros((SUB, LANES), jnp.float32)
    apply_inverse(plan, kept, source, result, 0, 0, plan.held)
    again.wait()
    apply_inverse(plan, rest, source, result, plan.held, 0, plan.rows - plan.held)
    finish(plan, second, state, result)


def finish(plan, second, state, result):
    squares = jnp.zeros((SUB, LANES), jnp.float32)
    for t in range(plan.tiles):
        new = result[t * SUB:(t + 1) * SUB, :]
        delta = new - state[t * SUB:(t + 1) * SUB, :]
        squares = squares + delta * delta
        state[t * SUB:(t + 1) * SUB, :] = new
    state[pl.ds(pl.multiple_of(plan.norm + second * SUB, SUB), SUB), :] = squares


def prepare_kernel(plan):
    rows, pad, neigh = plan.rows, plan.pad, plan.neigh

    def kernel(rhs, weights, neighbours, lists, inverse, kept, state, coupling, table,
               rhs_v, weights_v, slots_v, lists_v, rest, source, result, sems, part_sems):
        moves = ((rhs, rhs_v), (neighbours, slots_v), (weights, weights_v), (lists, lists_v))
        copies = [pltpu.make_async_copy(a, b, sems.at[n]) for n, (a, b) in enumerate(moves)]
        parts = [piece_copy(plan, n, inverse, kept, rest, part_sems.at[n]) for n in range(CHUNKS + 1)]
        for c in copies + parts:
            c.start()
        odd_x = lax.axis_index("gx") & 1
        odd_y = lax.axis_index("gy") & 1
        state[...] = jnp.zeros(state.shape, jnp.float32)
        result[pad - SUB:pad, :] = jnp.zeros((SUB, LANES), jnp.float32)
        table[...] = jnp.zeros(table.shape, jnp.int32)
        for c in copies:
            c.wait()
        state[plan.rhs:plan.rhs + rows, :] = rhs_v[:, 0, :]
        source[...] = state[plan.rhs:plan.rhs + pad, :].astype(jnp.bfloat16).astype(jnp.float32)

        slots = slots_v[...]
        group = (slots - plan.faces) // plan.halo
        within = (slots - plan.faces) & (plan.halo - 1)
        along_y = (group >= 2).astype(jnp.int32)
        side = ((group & 1) + 1 + jnp.where(group >= 2, odd_y, odd_x)) & 1
        place = jnp.where(slots < plan.faces, slots, plan.faces * (1 + along_y) + within + plan.halo * side)
        size = 3 * LANES
        where = lax.broadcasted_iota(jnp.int32, (size, LANES), 0)
        total = jnp.zeros((size, LANES), jnp.float32)
        for k in range(neigh):
            total = total + jnp.where(where == place[k:k + 1, :], weights_v[k:k + 1, :], 0.0)
        coupling[0:size, :], coupling[size:2 * size, :] = parts_of(total)

        both = jnp.concatenate([lists_v[...], lists_v[...]], axis=1)
        for n, odd in ((0, odd_x), (2, odd_y)):
            table[n:n + 1, :] = jnp.where(odd == 0, both[n:n + 1], both[n + 1:n + 2])
            table[n + 1:n + 2, :] = jnp.where(odd == 0, both[n + 1:n + 2], both[n:n + 1])

        for n, (start, stop) in enumerate(pieces(plan)):
            parts[n].wait()
            if n < CHUNKS:
                apply_inverse(plan, kept, source, result, 0, start, stop)
            else:
                apply_inverse(plan, rest, source, result, start, 0, stop - start)
        finish(plan, 0, state, result)

    def call(rhs, weights, neighbours, lists, inverse):
        return pl.pallas_call(
            kernel,
            name="prepare",
            in_specs=[pl.BlockSpec(memory_space=pltpu.HBM)] * 5,
            out_specs=[VSPEC] * 4,
            out_shape=[
                plan.held_type(inverse),
                plan.state_type,
                pltpu.VMEM((6 * LANES, LANES), jnp.bfloat16),
                pltpu.VMEM((SUB, LANES), jnp.int32),
            ],
            compiler_params=pltpu.CompilerParams(vmem_limit_bytes=VMEM_LIMIT),
            scratch_shapes=[
                pltpu.VMEM(rhs.shape, rhs.dtype),
                pltpu.VMEM(weights.shape, weights.dtype),
                pltpu.VMEM(neighbours.shape, neighbours.dtype),
                pltpu.VMEM(lists.shape, lists.dtype),
                plan.rest_type(inverse),
                pltpu.VMEM((pad, LANES), jnp.float32),
                pltpu.VMEM((pad, LANES), jnp.float32),
                pltpu.SemaphoreType.DMA((4,)),
                pltpu.SemaphoreType.DMA((CHUNKS + 1,)),
            ],
        )(*(hbm(v) for v in (rhs, weights, neighbours, lists, inverse)))

    return call


def begin_kernel(plan):
    def kernel(color, color_x, color_y, old_state, table, code, control, state, xe, xo, ye, yo, cx, cy, sems):
        del old_state
        copies = [pltpu.make_async_copy(a, b, sems.at[n]) for n, (a, b) in enumerate(((color_x, cx), (color_y, cy)))]
        for c in copies:
            c.start()
        odd_x = lax.axis_index("gx") & 1
        odd_y = lax.axis_index("gy") & 1
        for c in copies:
            c.wait()
        mine, beside_x, beside_y = color[0, 0], cx[0, 0], cy[0, 0]
        across = 6 - mine - beside_x - beside_y
        to_x = jnp.logical_or(beside_x == 0, across == 0).astype(jnp.int32)
        to_y = jnp.logical_or(beside_y == 0, across == 0).astype(jnp.int32)
        zero_x, zero_y = odd_x ^ to_x, odd_y ^ to_y
        opposite = jnp.where(to_x == 0, jnp.where(to_y == 0, across, beside_x), jnp.where(to_y == 0, beside_y, mine))
        next_x = jnp.where(to_x == 0, jnp.where(to_y == 0, beside_x, across), jnp.where(to_y == 0, mine, beside_y))
        chain = opposite == 2
        first = jnp.where(chain, mine, jnp.where(opposite == 1, mine >> 1, (mine + 1) >> 1))
        control[FIRST] = first
        control[SECOND] = first + jnp.where(chain, 4, 2)
        red = zero_x ^ zero_y
        total = 0
        for n in range(7):
            step = n >> 1 & 1
            alternate = jnp.where(n < jnp.where(opposite == 1, 3, 4), 5 + (red ^ (n & 1)), 0)
            axis_x = 1 + 2 * (zero_x ^ step)
            axis_y = 2 + 2 * (zero_y ^ step)
            around = jnp.where((next_x == 1) == (n % 2 == 0), axis_x, axis_y)
            total = total + (jnp.where(chain, around, alternate) << (4 * n))
        code[0] = total

        @pl.when(first != 0)
        def _():
            state[0:plan.pad, :] = jnp.zeros((plan.pad, LANES), jnp.float32)
            state[plan.norm:plan.norm + SUB, :] = jnp.zeros((SUB, LANES), jnp.float32)

        for n, ref in enumerate((xe, xo, ye, yo)):
            write_pack(plan, state, table, n, ref)

    def call(color, color_x, color_y, state, table):
        return pl.pallas_call(
            kernel,
            name="begin",
            in_specs=[SSPEC] + [pl.BlockSpec(memory_space=pl.ANY)] * 2 + [VSPEC] * 2,
            out_specs=[SSPEC] * 2 + [VSPEC] * 5,
            out_shape=[pltpu.SMEM((1,), jnp.int32), plan.control_type, plan.state_type] + [plan.pack_type] * 4,
            input_output_aliases={3: 2},
            compiler_params=pltpu.CompilerParams(vmem_limit_bytes=VMEM_LIMIT),
            scratch_shapes=[
                pltpu.SMEM(color.shape, color.dtype),
                pltpu.SMEM(color.shape, color.dtype),
                pltpu.SemaphoreType.DMA((2,)),
            ],
        )(color, color_x, color_y, vmem(state), vmem(table))

    return call


def merge_kernel(plan, name, receives, steps):
    def kernel(*refs):
        old_state, *got = refs[:-1]
        state = refs[-1]
        del old_state
        place = (lax.axis_index("gx"), lax.axis_index("gy"))

        @pl.when(receives(place[0] & 1, place[1] & 1))
        def _():
            for axis in sorted({axis for axis, _ in steps}):
                even, odd = (got[steps.index((axis, n))] for n in (0, 1))
                there = jnp.logical_and(place[axis] > 0, place[axis] < (plan.nx, plan.ny)[axis] - 1)
                merge(plan, state, plan.along[axis], even, odd, there)

    def call(state, got):
        return pl.pallas_call(
            kernel,
            name=name,
            in_specs=[VSPEC] * (1 + len(got)),
            out_specs=VSPEC,
            out_shape=plan.state_type,
            input_output_aliases={0: 0},
            compiler_params=pltpu.CompilerParams(vmem_limit_bytes=VMEM_LIMIT),
        )(*(vmem(v) for v in (state, *got)))

    return call


def level_kernel(plan):
    def kernel(control, old_state, coupling, table, kept, inverse, state, xe, xo, ye, yo, rest, source, result, sem):
        del old_state
        steps = state[plan.step:plan.step + SUB, :] + 1.0
        state[plan.step:plan.step + SUB, :] = steps
        step = steps[0, 0].astype(jnp.int32)
        second = (step == control[SECOND]).astype(jnp.int32)
        turn = jnp.logical_or(step == control[FIRST], step == control[SECOND])

        @pl.when(turn)
        def _():
            update(plan, second, state, coupling, inverse, kept, rest, source, result, sem)

        for n, ref in enumerate((xe, xo, ye, yo)):
            write_pack(plan, state, table, n, ref)

    def call(control, state, coupling, table, kept, inverse):
        return pl.pallas_call(
            kernel,
            name="level",
            in_specs=[SSPEC] + [VSPEC] * 4 + [pl.BlockSpec(memory_space=pltpu.HBM)],
            out_specs=[VSPEC] * 5,
            out_shape=[plan.state_type] + [plan.pack_type] * 4,
            input_output_aliases={1: 0},
            compiler_params=pltpu.CompilerParams(vmem_limit_bytes=VMEM_LIMIT),
            scratch_shapes=[
                plan.rest_type(inverse),
                pltpu.VMEM((plan.pad, LANES), jnp.float32),
                pltpu.VMEM((plan.pad, LANES), jnp.float32),
                pltpu.SemaphoreType.DMA,
            ],
        )(smem(control), *(vmem(v) for v in (state, coupling, table, kept)), hbm(inverse))

    return call


def last_kernel(plan):
    devices = plan.nx * plan.ny

    def kernel(state, out, sums):
        out[:, 0, :] = state[0:plan.rows, :]
        lane = lax.broadcasted_iota(jnp.int32, (devices, LANES), 1)
        first = jnp.sum(state[plan.norm:plan.norm + SUB, :])
        second = jnp.sum(state[plan.norm + SUB:plan.norm + 2 * SUB, :])
        sums[...] = jnp.where(lane == 0, first, jnp.where(lane == 1, second, 0.0))

    def call(state):
        return pl.pallas_call(
            kernel,
            name="last",
            in_specs=[VSPEC],
            out_specs=[VSPEC] * 2,
            out_shape=[
                jax.ShapeDtypeStruct((plan.rows, 1, LANES), jnp.float32),
                pltpu.VMEM((devices, LANES), jnp.float32),
            ],
            compiler_params=pltpu.CompilerParams(vmem_limit_bytes=VMEM_LIMIT),
        )(vmem(state))

    return call


def edge_pairs(plan, axis, odd, sends, both):
    pairs = []
    for i in range(plan.nx):
        for j in range(plan.ny):
            step = 1 if (i, j)[axis] % 2 == odd else -1
            u, v = (i + step, j) if axis == 0 else (i, j + step)
            if 0 <= u < plan.nx and 0 <= v < plan.ny and (both or sends(i, j)):
                pairs.append((i * plan.ny + j, u * plan.ny + v))
    return pairs


def circle_pairs(plan, axis, parity):
    pairs = []

    def number(at):
        return at[0] * plan.ny + at[1]

    for i in range(plan.nx):
        for j in range(plan.ny):
            here = [i, j]
            ahead = 1 if here[axis] % 2 == 1 else -1
            inside = 0 <= here[axis] + ahead < (plan.nx, plan.ny)[axis]
            to = list(here)
            if inside:
                to[axis] += ahead
            if here[axis] % 2 != parity or not inside:
                to[1 - axis] ^= 1
            pairs.append((number(here), number(to)))
    return pairs


def flow(plan, name, axes, parity):
    steps = [(axis, odd) for axis in (1, 0) if axis in axes for odd in (1, 0)]

    def sends(i, j):
        return (i * (0 in axes) + j * (1 in axes)) % 2 == parity

    def receives(i, j):
        return ((i if axes == (0,) else j if axes == (1,) else i ^ j) & 1) != parity

    def run(state, *packs):
        got = []
        for n, (axis, odd) in enumerate(steps):
            if len(axes) == 1 and odd:
                pairs = circle_pairs(plan, axis, parity)
            else:
                pairs = edge_pairs(plan, axis, odd, sends, n == len(steps) - 1)
            got.append(lax.ppermute(packs[2 * axis + odd], ("gx", "gy"), pairs))
        return merge_kernel(plan, name, receives, steps)(state, got)

    return run


def body_for(mesh):
    def body(rhs, inverse, weights, neighbours, send_lists, coloring):
        rows, faces = rhs.shape[1:]
        plan = Plan(mesh, rows, faces, send_lists.shape[2], weights.shape[1])
        color_x = lax.ppermute(coloring, "gx", [(i, i ^ 1) for i in range(plan.nx)])
        color_y = lax.ppermute(coloring, "gy", [(j, j ^ 1) for j in range(plan.ny)])
        kept, state, coupling, table = prepare_kernel(plan)(
            rhs.transpose(1, 0, 2), weights[0], neighbours[0], send_lists[0], inverse[0])
        code, control, state, *packs = begin_kernel(plan)(coloring, color_x, color_y, state, table)
        flows = [
            flow(plan, f"along_{'xy'[axis]}{parity}", (axis,), parity)
            for parity in (0, 1) for axis in (0, 1)
        ]
        flows += [flow(plan, f"both{parity}", (0, 1), parity) for parity in (0, 1)]

        def turn(carry):
            code, state, packs = carry
            state = lax.switch((code & 7) - 1, flows, state, *packs)
            state, *packs = level_kernel(plan)(control, state, coupling, table, kept, inverse[0])
            return code >> 4, state, tuple(packs)

        state = lax.while_loop(lambda carry: carry[0] != 0, turn, (code[0], state, tuple(packs)))[1]
        out, sums = last_kernel(plan)(state)
        sums = lax.all_to_all(sums, ("gx", "gy"), 0, 0, tiled=True)
        norms = jnp.sqrt(jnp.sum(sums[:, :2], axis=0))
        return out.transpose(1, 0, 2), norms

    return body


def solution(mesh):
    in_specs = (
        P("gx", None, "gy"),
        P("gx", None, None, "gy"),
        P("gx", None, "gy"),
        P("gx", None, "gy"),
        P("gx", None, "gy"),
        P("gx", "gy"),
    )
    out_specs = (P("gx", None, "gy"), P())
    return jax.shard_map(body_for(mesh), mesh=mesh, in_specs=in_specs, out_specs=out_specs, check_vma=False)
```

profile of v0, /device:TPU:0, one launch (start us, length us, event | category | flops | bytes accessed | tf_op | source)
XLA Modules:
  0.0 61.4 jit_solution(3763001202509146975)
XLA Ops:
  0.6 0.6 collective-permute-start.16
  1.2 2.6 %collective-permute-start.17 = (s32[1,1]{1,0:T(1,128)}, s32[1,1]{1,0:T(1,128)}, u32[]{:S(2)}, u32[]{:S(2)}) collective-permute-start(s32[1,1]{1,0:T(1,128)} %param.19), channel_id=1, source_target_pairs={{0,1},{1,0},{2,3},{3,2},{4,5},{5,4},{6,7},{7,6},{8,9},{9,8},{10,11... | collective-permute-start | bytes 20 | tf_op jit(solution)/shard_map/ppermute | solution.py:422
  4.5 2.9 %prepare.1 = (bf16[90,125,128]{2,1,0:T(8,128)(2,1)S(1)}, f32[536,128]{1,0:T(8,128)S(1)}, bf16[768,128]{1,0:T(8,128)(2,1)S(1)}, s32[8,128]{1,0:T(8,128)S(1)}) custom-call(f32[125,1,128]{2,1,0:T(1,128)} %bitcast.18, f32[4,128]{1,0:T(4,128)} %bitcast.19, s32[4,128]{1,0:T(4,128)} %bitcast.20, s32[4,64]{1,0:T(4,128)} %bitcast.21, bf16[125,125,128]{2,1,0:T(8,128)(2,1)} %bitcast.15), custom_call_target="tpu_custom_call" | custom-call | tf_op jit(solution)/shard_map/prepare/pallas_call | solution.py:187
  7.5 2.1 %begin.1 = (s32[1]{0:T(128)S(4)}, s32[2]{0:T(128)S(4)}, f32[536,128]{1,0:T(8,128)S(1)}, f32[64,128]{1,0:T(8,128)S(1)}, f32[64,128]{1,0:T(8,128)S(1)}, /*index=5*/f32[64,128]{1,0:T(8,128)S(1)}, f32[64,128]{1,0:T(8,128)S(1)}) custom-call(s32[1,1]{1,0:T(1,128)S(6)} %copy.49.color, ...), custom_call_target="tpu_custom_call", output_to_operand_aliasing={{2}: (3, {})} | custom-call | tf_op jit(solution)/shard_map/begin/pallas_call | solution.py:256
  9.5 37.2 %while.20 = (s32[]{:T(128)S(4)}, f32[536,128]{1,0:T(8,128)S(1)}, f32[64,128]{1,0:T(8,128)S(1)}, f32[64,128]{1,0:T(8,128)S(1)}, f32[64,128]{1,0:T(8,128)S(1)}, /*...) while((s32[]{:T(128)S(4)}, f32[536,128]{1,0:T(8,128)S(1)}, ...), condition=%wide.region_7.0_spmd, body=%wide.region_0.0_spmd.sunk | while | flops 5 | bytes 524733 | solution.py:438
  9.6 5.2 %conditional.2 = (f32[536,128]{1,0:T(8,128)S(1)}) conditional(s32[]{:T(128)} %clamp.7, (f32[64,128]{1,0:T(8,128)S(1)}, f32[64,128]{1,0:T(8,128)S(1)}, f32[536,128]{1,0:T(8,128)S(1)}) %tuple.51, (f32[64,128]{1,0:T(8,128)S(1)}, f32[64,128]{1,0:T(8,128)S(1)}, f32[536,128]{1,0:T(8,128)S(1)}) %tuple.52, ...), branch_computations={%region_1.0_spmd, %region_2.0_spmd, %region_3.0_spmd, %region_4.0_... | conditional | bytes 524456 | solution.py:434
  9.8 3.0 %collective-permute-start.7 = (f32[64,128]{1,0:T(8,128)S(1)}, f32[64,128]{1,0:T(8,128)S(1)}, u32[]{:S(2)}, u32[]{:S(2)}) collective-permute-start(f32[64,128]{1,0:T(8,128)S(1)} %get-tuple-element.192), channel_id=1, source_target_pairs={{0,1},{1,0},{2,3},{3,2},{4,5},{5,4},{6,7},{7,6},{8,9},{9,8},{10,11... | collective-permute-start | bytes 98312 | tf_op jit(solution)/shard_map/while/body/cond/branch_3_fun/ppermute | solution.py:411
  12.8 1.9 %collective-permute-done.7.refs_2_ = f32[64,128]{1,0:T(8,128)S(1)} collective-permute-done((f32[64,128]{1,0:T(8,128)S(1)}, f32[64,128]{1,0:T(8,128)S(1)}, u32[]{:S(2)}, u32[]{:S(2)}) %collective-permute-start.7) | collective-permute-done | bytes 32800 | tf_op jit(solution)/shard_map/while/body/cond/branch_3_fun/ppermute | solution.py:411
  15.1 4.1 %conditional.2 = (f32[536,128]{1,0:T(8,128)S(1)}) conditional(s32[]{:T(128)} %clamp.7, (f32[64,128]{1,0:T(8,128)S(1)}, f32[64,128]{1,0:T(8,128)S(1)}, f32[536,128]{1,0:T(8,128)S(1)}) %tuple.51, (f32[64,128]{1,0:T(8,128)S(1)}, f32[64,128]{1,0:T(8,128)S(1)}, f32[536,128]{1,0:T(8,128)S(1)}) %tuple.52, ...), branch_computations={%region_1.0_spmd, %region_2.0_spmd, %region_3.0_spmd, %region_4.0_... | conditional | bytes 524456 | solution.py:434
  15.1 2.0 %collective-permute-start.4 = (f32[64,128]{1,0:T(8,128)S(1)}, f32[64,128]{1,0:T(8,128)S(1)}, u32[]{:S(2)}, u32[]{:S(2)}) collective-permute-start(f32[64,128]{1,0:T(8,128)S(1)} %get-tuple-element.188), channel_id=1, source_target_pairs={{0,1},{1,0},{2,3},{3,2},{4,8},{5,9},{6,10},{7,11},{8,5},{9,4},{10,... | collective-permute-start | bytes 98312 | tf_op jit(solution)/shard_map/while/body/cond/branch_2_fun/ppermute | solution.py:411
  17.1 2.0 %collective-permute-done.4.refs_1_ = f32[64,128]{1,0:T(8,128)S(1)} collective-permute-done((f32[64,128]{1,0:T(8,128)S(1)}, f32[64,128]{1,0:T(8,128)S(1)}, u32[]{:S(2)}, u32[]{:S(2)}) %collective-permute-start.4) | collective-permute-done | bytes 32800 | tf_op jit(solution)/shard_map/while/body/cond/branch_2_fun/ppermute | solution.py:411
  19.2 1.8 %level.4 = (f32[536,128]{1,0:T(8,128)S(1)}, f32[64,128]{1,0:T(8,128)S(1)}, f32[64,128]{1,0:T(8,128)S(1)}, f32[64,128]{1,0:T(8,128)S(1)}, f32[64,128]{1,0:T(8,128)S(1)}) custom-call(s32[2]{0:T(128)S(4)} %get-tuple-element.388.control, f32[536,128]{1,0:T(8,128)S(1)} %get-tuple-element.397.old_state, ...), custom_call_target="tpu_custom_call", output_to_operand_aliasing={{0}: (1, {})} | custom-call | tf_op jit(solution)/shard_map/while/body/level/pallas_call | solution.py:319
  21.1 4.1 %conditional.2 = (f32[536,128]{1,0:T(8,128)S(1)}) conditional(s32[]{:T(128)} %clamp.7, (f32[64,128]{1,0:T(8,128)S(1)}, f32[64,128]{1,0:T(8,128)S(1)}, f32[536,128]{1,0:T(8,128)S(1)}) %tuple.51, (f32[64,128]{1,0:T(8,128)S(1)}, f32[64,128]{1,0:T(8,128)S(1)}, f32[536,128]{1,0:T(8,128)S(1)}) %tuple.52, ...), branch_computations={%region_1.0_spmd, %region_2.0_spmd, %region_3.0_spmd, %region_4.0_... | conditional | bytes 524456 | solution.py:434
  21.1 0.9 %collective-permute-start.3 = (f32[64,128]{1,0:T(8,128)S(1)}, f32[64,128]{1,0:T(8,128)S(1)}, u32[]{:S(2)}, u32[]{:S(2)}) collective-permute-start(f32[64,128]{1,0:T(8,128)S(1)} %get-tuple-element.186), channel_id=1, source_target_pairs={{0,1},{1,0},{2,3},{3,2},{4,5},{5,4},{6,7},{7,6},{8,9},{9,8},{10,11... | collective-permute-start | bytes 98312 | tf_op jit(solution)/shard_map/while/body/cond/branch_1_fun/ppermute | solution.py:411
  22.3 2.8 %collective-permute-done.3.refs_2_ = f32[64,128]{1,0:T(8,128)S(1)} collective-permute-done((f32[64,128]{1,0:T(8,128)S(1)}, f32[64,128]{1,0:T(8,128)S(1)}, u32[]{:S(2)}, u32[]{:S(2)}) %collective-permute-start.3) | collective-permute-done | bytes 32800 | tf_op jit(solution)/shard_map/while/body/cond/branch_1_fun/ppermute | solution.py:411
  25.4 5.4 %conditional.2 = (f32[536,128]{1,0:T(8,128)S(1)}) conditional(s32[]{:T(128)} %clamp.7, (f32[64,128]{1,0:T(8,128)S(1)}, f32[64,128]{1,0:T(8,128)S(1)}, f32[536,128]{1,0:T(8,128)S(1)}) %tuple.51, (f32[64,128]{1,0:T(8,128)S(1)}, f32[64,128]{1,0:T(8,128)S(1)}, f32[536,128]{1,0:T(8,128)S(1)}) %tuple.52, ...), branch_computations={%region_1.0_spmd, %region_2.0_spmd, %region_3.0_spmd, %region_4.0_... | conditional | bytes 524456 | solution.py:434
  25.4 2.7 %collective-permute-start = (f32[64,128]{1,0:T(8,128)S(1)}, f32[64,128]{1,0:T(8,128)S(1)}, u32[]{:S(2)}, u32[]{:S(2)}) collective-permute-start(f32[64,128]{1,0:T(8,128)S(1)} %get-tuple-element.182), channel_id=1, source_target_pairs={{0,1},{1,0},{2,3},{3,2},{4,9},{5,8},{6,11},{7,10},{8,4},{9,5},{10,... | collective-permute-start | bytes 98312 | tf_op jit(solution)/shard_map/while/body/cond/branch_0_fun/ppermute | solution.py:411
  28.1 1.9 %collective-permute-start.1 = (f32[64,128]{1,0:T(8,128)S(1)}, f32[64,128]{1,0:T(8,128)S(1)}, u32[]{:S(2)}, u32[]{:S(2)}) collective-permute-start(f32[64,128]{1,0:T(8,128)S(1)} %get-tuple-element.183), channel_id=1, source_target_pairs={{0,4},{1,5},{2,6},{3,7},{4,0},{5,1},{6,2},{7,3},{8,12},{9,13},{10,... | collective-permute-start | bytes 98312 | tf_op jit(solution)/shard_map/while/body/cond/branch_0_fun/ppermute | solution.py:411
  30.1 0.7 %collective-permute-done.1.refs_2_ = f32[64,128]{1,0:T(8,128)S(1)} collective-permute-done((f32[64,128]{1,0:T(8,128)S(1)}, f32[64,128]{1,0:T(8,128)S(1)}, u32[]{:S(2)}, u32[]{:S(2)}) %collective-permute-start.1) | collective-permute-done | bytes 32800 | tf_op jit(solution)/shard_map/while/body/cond/branch_0_fun/ppermute | solution.py:411
  31.1 4.8 %conditional.2 = (f32[536,128]{1,0:T(8,128)S(1)}) conditional(s32[]{:T(128)} %clamp.7, (f32[64,128]{1,0:T(8,128)S(1)}, f32[64,128]{1,0:T(8,128)S(1)}, f32[536,128]{1,0:T(8,128)S(1)}) %tuple.51, (f32[64,128]{1,0:T(8,128)S(1)}, f32[64,128]{1,0:T(8,128)S(1)}, f32[536,128]{1,0:T(8,128)S(1)}) %tuple.52, ...), branch_computations={%region_1.0_spmd, %region_2.0_spmd, %region_3.0_spmd, %region_4.0_... | conditional | bytes 524456 | solution.py:434
  31.7 0.8 %collective-permute-start.7 = (f32[64,128]{1,0:T(8,128)S(1)}, f32[64,128]{1,0:T(8,128)S(1)}, u32[]{:S(2)}, u32[]{:S(2)}) collective-permute-start(f32[64,128]{1,0:T(8,128)S(1)} %get-tuple-element.192), channel_id=1, source_target_pairs={{0,1},{1,0},{2,3},{3,2},{4,5},{5,4},{6,7},{7,6},{8,9},{9,8},{10,11... | collective-permute-start | bytes 98312 | tf_op jit(solution)/shard_map/while/body/cond/branch_3_fun/ppermute | solution.py:411
  32.5 3.3 %collective-permute-done.7.refs_2_ = f32[64,128]{1,0:T(8,128)S(1)} collective-permute-done((f32[64,128]{1,0:T(8,128)S(1)}, f32[64,128]{1,0:T(8,128)S(1)}, u32[]{:S(2)}, u32[]{:S(2)}) %collective-permute-start.7) | collective-permute-done | bytes 32800 | tf_op jit(solution)/shard_map/while/body/cond/branch_3_fun/ppermute | solution.py:411
  36.2 4.1 %conditional.2 = (f32[536,128]{1,0:T(8,128)S(1)}) conditional(s32[]{:T(128)} %clamp.7, (f32[64,128]{1,0:T(8,128)S(1)}, f32[64,128]{1,0:T(8,128)S(1)}, f32[536,128]{1,0:T(8,128)S(1)}) %tuple.51, (f32[64,128]{1,0:T(8,128)S(1)}, f32[64,128]{1,0:T(8,128)S(1)}, f32[536,128]{1,0:T(8,128)S(1)}) %tuple.52, ...), branch_computations={%region_1.0_spmd, %region_2.0_spmd, %region_3.0_spmd, %region_4.0_... | conditional | bytes 524456 | solution.py:434
  36.7 1.3 %collective-permute-start.5 = (f32[64,128]{1,0:T(8,128)S(1)}, f32[64,128]{1,0:T(8,128)S(1)}, u32[]{:S(2)}, u32[]{:S(2)}) collective-permute-start(f32[64,128]{1,0:T(8,128)S(1)} %get-tuple-element.189), channel_id=1, source_target_pairs={{0,4},{1,5},{2,6},{3,7},{4,0},{5,1},{6,2},{7,3},{8,12},{9,13},{10,... | collective-permute-start | bytes 98312 | tf_op jit(solution)/shard_map/while/body/cond/branch_2_fun/ppermute | solution.py:411
  38.0 2.2 %collective-permute-done.4.refs_1_ = f32[64,128]{1,0:T(8,128)S(1)} collective-permute-done((f32[64,128]{1,0:T(8,128)S(1)}, f32[64,128]{1,0:T(8,128)S(1)}, u32[]{:S(2)}, u32[]{:S(2)}) %collective-permute-start.4) | collective-permute-done | bytes 32800 | tf_op jit(solution)/shard_map/while/body/cond/branch_2_fun/ppermute | solution.py:411
  40.3 1.8 %level.4 = (f32[536,128]{1,0:T(8,128)S(1)}, f32[64,128]{1,0:T(8,128)S(1)}, f32[64,128]{1,0:T(8,128)S(1)}, f32[64,128]{1,0:T(8,128)S(1)}, f32[64,128]{1,0:T(8,128)S(1)}) custom-call(s32[2]{0:T(128)S(4)} %get-tuple-element.388.control, f32[536,128]{1,0:T(8,128)S(1)} %get-tuple-element.397.old_state, ...), custom_call_target="tpu_custom_call", output_to_operand_aliasing={{0}: (1, {})} | custom-call | tf_op jit(solution)/shard_map/while/body/level/pallas_call | solution.py:319
  42.2 4.3 %conditional.2 = (f32[536,128]{1,0:T(8,128)S(1)}) conditional(s32[]{:T(128)} %clamp.7, (f32[64,128]{1,0:T(8,128)S(1)}, f32[64,128]{1,0:T(8,128)S(1)}, f32[536,128]{1,0:T(8,128)S(1)}) %tuple.51, (f32[64,128]{1,0:T(8,128)S(1)}, f32[64,128]{1,0:T(8,128)S(1)}, f32[536,128]{1,0:T(8,128)S(1)}) %tuple.52, ...), branch_computations={%region_1.0_spmd, %region_2.0_spmd, %region_3.0_spmd, %region_4.0_... | conditional | bytes 524456 | solution.py:434
  42.6 1.1 %collective-permute-start.3 = (f32[64,128]{1,0:T(8,128)S(1)}, f32[64,128]{1,0:T(8,128)S(1)}, u32[]{:S(2)}, u32[]{:S(2)}) collective-permute-start(f32[64,128]{1,0:T(8,128)S(1)} %get-tuple-element.186), channel_id=1, source_target_pairs={{0,1},{1,0},{2,3},{3,2},{4,5},{5,4},{6,7},{7,6},{8,9},{9,8},{10,11... | collective-permute-start | bytes 98312 | tf_op jit(solution)/shard_map/while/body/cond/branch_1_fun/ppermute | solution.py:411
  43.7 2.8 %collective-permute-done.3.refs_2_ = f32[64,128]{1,0:T(8,128)S(1)} collective-permute-done((f32[64,128]{1,0:T(8,128)S(1)}, f32[64,128]{1,0:T(8,128)S(1)}, u32[]{:S(2)}, u32[]{:S(2)}) %collective-permute-start.3) | collective-permute-done | bytes 32800 | tf_op jit(solution)/shard_map/while/body/cond/branch_1_fun/ppermute | solution.py:411
  46.7 0.7 %last.1 = (f32[125,1,128]{2,1,0:T(1,128)}, f32[32,128]{1,0:T(8,128)S(1)}) custom-call(f32[536,128]{1,0:T(8,128)S(1)} %get-tuple-element.247.state), custom_call_target="tpu_custom_call" | custom-call | tf_op jit(solution)/shard_map/last/pallas_call | solution.py:349
  47.4 13.5 %all_to_all.12 = f32[32,1,128]{2,1,0:T(1,128)S(1)} all-to-all(f32[32,1,128]{2,1,0:T(1,128)S(1)} %bitcast.14), channel_id=1, replica_groups=mesh['gx'=8,'gy'=4] {'gx','gy'}, dimensions={0} | all-to-all | bytes 32768 | tf_op jit(solution)/shard_map/all_to_all | solution.py:440
  60.9 0.5 sqrt.3
  (28 shorter events, 3.4 us)
Async XLA Ops:
  0.6 6.8 %collective-permute-start.16 = (s32[1,1]{1,0:T(1,128)}, s32[1,1]{1,0:T(1,128)}, u32[]{:S(2)}, u32[]{:S(2)}) collective-permute-start(s32[1,1]{1,0:T(1,128)} %param.19), channel_id=1, source_target_pairs={{0,4},{4,0},{8,12},{12,8},{16,20},{20,16},{24,28},{28,24},{1,5},{5... | collective-permute-start | bytes 20 | tf_op jit(solution)/shard_map/ppermute | solution.py:421
  1.2 6.3 %collective-permute-start.17 = (s32[1,1]{1,0:T(1,128)}, s32[1,1]{1,0:T(1,128)}, u32[]{:S(2)}, u32[]{:S(2)}) collective-permute-start(s32[1,1]{1,0:T(1,128)} %param.19), channel_id=1, source_target_pairs={{0,1},{1,0},{2,3},{3,2},{4,5},{5,4},{6,7},{7,6},{8,9},{9,8},{10,11... | collective-permute-start | bytes 20 | tf_op jit(solution)/shard_map/ppermute | solution.py:422
  9.6 3.2 %collective-permute-start.6 = (f32[64,128]{1,0:T(8,128)S(1)}, f32[64,128]{1,0:T(8,128)S(1)}, u32[]{:S(2)}, u32[]{:S(2)}) collective-permute-start(f32[64,128]{1,0:T(8,128)S(1)} %get-tuple-element.191), channel_id=1, source_target_pairs={{0,4},{1,2},{2,5},{3,7},{4,0},{5,6},{6,1},{7,3},{8,12},{9,10},{10,... | collective-permute-start | bytes 98312 | tf_op jit(solution)/shard_map/while/body/cond/branch_3_fun/ppermute | solution.py:411
  9.8 4.9 %collective-permute-start.7 = (f32[64,128]{1,0:T(8,128)S(1)}, f32[64,128]{1,0:T(8,128)S(1)}, u32[]{:S(2)}, u32[]{:S(2)}) collective-permute-start(f32[64,128]{1,0:T(8,128)S(1)} %get-tuple-element.192), channel_id=1, source_target_pairs={{0,1},{1,0},{2,3},{3,2},{4,5},{5,4},{6,7},{7,6},{8,9},{9,8},{10,11... | collective-permute-start | bytes 98312 | tf_op jit(solution)/shard_map/while/body/cond/branch_3_fun/ppermute | solution.py:411
  15.1 4.0 %collective-permute-start.4 = (f32[64,128]{1,0:T(8,128)S(1)}, f32[64,128]{1,0:T(8,128)S(1)}, u32[]{:S(2)}, u32[]{:S(2)}) collective-permute-start(f32[64,128]{1,0:T(8,128)S(1)} %get-tuple-element.188), channel_id=1, source_target_pairs={{0,1},{1,0},{2,3},{3,2},{4,8},{5,9},{6,10},{7,11},{8,5},{9,4},{10,... | collective-permute-start | bytes 98312 | tf_op jit(solution)/shard_map/while/body/cond/branch_2_fun/ppermute | solution.py:411
  17.1 2.0 %collective-permute-start.5 = (f32[64,128]{1,0:T(8,128)S(1)}, f32[64,128]{1,0:T(8,128)S(1)}, u32[]{:S(2)}, u32[]{:S(2)}) collective-permute-start(f32[64,128]{1,0:T(8,128)S(1)} %get-tuple-element.189), channel_id=1, source_target_pairs={{0,4},{1,5},{2,6},{3,7},{4,0},{5,1},{6,2},{7,3},{8,12},{9,13},{10,... | collective-permute-start | bytes 98312 | tf_op jit(solution)/shard_map/while/body/cond/branch_2_fun/ppermute | solution.py:411
  21.1 1.3 %collective-permute-start.2 = (f32[64,128]{1,0:T(8,128)S(1)}, f32[64,128]{1,0:T(8,128)S(1)}, u32[]{:S(2)}, u32[]{:S(2)}) collective-permute-start(f32[64,128]{1,0:T(8,128)S(1)} %get-tuple-element.185), channel_id=1, source_target_pairs={{0,4},{1,6},{2,1},{3,7},{4,0},{5,2},{6,5},{7,3},{8,12},{9,14},{10,... | collective-permute-start | bytes 98312 | tf_op jit(solution)/shard_map/while/body/cond/branch_1_fun/ppermute | solution.py:411
  21.1 4.0 %collective-permute-start.3 = (f32[64,128]{1,0:T(8,128)S(1)}, f32[64,128]{1,0:T(8,128)S(1)}, u32[]{:S(2)}, u32[]{:S(2)}) collective-permute-start(f32[64,128]{1,0:T(8,128)S(1)} %get-tuple-element.186), channel_id=1, source_target_pairs={{0,1},{1,0},{2,3},{3,2},{4,5},{5,4},{6,7},{7,6},{8,9},{9,8},{10,11... | collective-permute-start | bytes 98312 | tf_op jit(solution)/shard_map/while/body/cond/branch_1_fun/ppermute | solution.py:411
  25.4 4.7 %collective-permute-start = (f32[64,128]{1,0:T(8,128)S(1)}, f32[64,128]{1,0:T(8,128)S(1)}, u32[]{:S(2)}, u32[]{:S(2)}) collective-permute-start(f32[64,128]{1,0:T(8,128)S(1)} %get-tuple-element.182), channel_id=1, source_target_pairs={{0,1},{1,0},{2,3},{3,2},{4,9},{5,8},{6,11},{7,10},{8,4},{9,5},{10,... | collective-permute-start | bytes 98312 | tf_op jit(solution)/shard_map/while/body/cond/branch_0_fun/ppermute | solution.py:411
  28.1 2.8 %collective-permute-start.1 = (f32[64,128]{1,0:T(8,128)S(1)}, f32[64,128]{1,0:T(8,128)S(1)}, u32[]{:S(2)}, u32[]{:S(2)}) collective-permute-start(f32[64,128]{1,0:T(8,128)S(1)} %get-tuple-element.183), channel_id=1, source_target_pairs={{0,4},{1,5},{2,6},{3,7},{4,0},{5,1},{6,2},{7,3},{8,12},{9,13},{10,... | collective-permute-start | bytes 98312 | tf_op jit(solution)/shard_map/while/body/cond/branch_0_fun/ppermute | solution.py:411
  31.1 1.4 %collective-permute-start.6 = (f32[64,128]{1,0:T(8,128)S(1)}, f32[64,128]{1,0:T(8,128)S(1)}, u32[]{:S(2)}, u32[]{:S(2)}) collective-permute-start(f32[64,128]{1,0:T(8,128)S(1)} %get-tuple-element.191), channel_id=1, source_target_pairs={{0,4},{1,2},{2,5},{3,7},{4,0},{5,6},{6,1},{7,3},{8,12},{9,10},{10,... | collective-permute-start | bytes 98312 | tf_op jit(solution)/shard_map/while/body/cond/branch_3_fun/ppermute | solution.py:411
  31.7 4.2 %collective-permute-start.7 = (f32[64,128]{1,0:T(8,128)S(1)}, f32[64,128]{1,0:T(8,128)S(1)}, u32[]{:S(2)}, u32[]{:S(2)}) collective-permute-start(f32[64,128]{1,0:T(8,128)S(1)} %get-tuple-element.192), channel_id=1, source_target_pairs={{0,1},{1,0},{2,3},{3,2},{4,5},{5,4},{6,7},{7,6},{8,9},{9,8},{10,11... | collective-permute-start | bytes 98312 | tf_op jit(solution)/shard_map/while/body/cond/branch_3_fun/ppermute | solution.py:411
  36.3 4.0 %collective-permute-start.4 = (f32[64,128]{1,0:T(8,128)S(1)}, f32[64,128]{1,0:T(8,128)S(1)}, u32[]{:S(2)}, u32[]{:S(2)}) collective-permute-start(f32[64,128]{1,0:T(8,128)S(1)} %get-tuple-element.188), channel_id=1, source_target_pairs={{0,1},{1,0},{2,3},{3,2},{4,8},{5,9},{6,10},{7,11},{8,5},{9,4},{10,... | collective-permute-start | bytes 98312 | tf_op jit(solution)/shard_map/while/body/cond/branch_2_fun/ppermute | solution.py:411
  36.7 3.5 %collective-permute-start.5 = (f32[64,128]{1,0:T(8,128)S(1)}, f32[64,128]{1,0:T(8,128)S(1)}, u32[]{:S(2)}, u32[]{:S(2)}) collective-permute-start(f32[64,128]{1,0:T(8,128)S(1)} %get-tuple-element.189), channel_id=1, source_target_pairs={{0,4},{1,5},{2,6},{3,7},{4,0},{5,1},{6,2},{7,3},{8,12},{9,13},{10,... | collective-permute-start | bytes 98312 | tf_op jit(solution)/shard_map/while/body/cond/branch_2_fun/ppermute | solution.py:411
  42.2 1.4 %collective-permute-start.2 = (f32[64,128]{1,0:T(8,128)S(1)}, f32[64,128]{1,0:T(8,128)S(1)}, u32[]{:S(2)}, u32[]{:S(2)}) collective-permute-start(f32[64,128]{1,0:T(8,128)S(1)} %get-tuple-element.185), channel_id=1, source_target_pairs={{0,4},{1,6},{2,1},{3,7},{4,0},{5,2},{6,5},{7,3},{8,12},{9,14},{10,... | collective-permute-start | bytes 98312 | tf_op jit(solution)/shard_map/while/body/cond/branch_1_fun/ppermute | solution.py:411
  42.6 3.9 %collective-permute-start.3 = (f32[64,128]{1,0:T(8,128)S(1)}, f32[64,128]{1,0:T(8,128)S(1)}, u32[]{:S(2)}, u32[]{:S(2)}) collective-permute-start(f32[64,128]{1,0:T(8,128)S(1)} %get-tuple-element.186), channel_id=1, source_target_pairs={{0,1},{1,0},{2,3},{3,2},{4,5},{5,4},{6,7},{7,6},{8,9},{9,8},{10,11... | collective-permute-start | bytes 98312 | tf_op jit(solution)/shard_map/while/body/cond/branch_1_fun/ppermute | solution.py:411
where the time goes:
time: 60.8 us; the launch traced here: 61.4 us
  starting transfers between devices  18.4 us (30%)
  waiting for transfers between devices  16.2 us (27%)
  blocking collectives  13.5 us (22%)
  Pallas kernels  10.6 us (17%)
  between operations  1.36 us (2%)
  loops' own time  0.84 us (1%)
    ppermute x14, waiting for transfers between devices, run(): got.append(lax.ppermute(packs[2 * axis + odd], ('gx', 'gy'), pairs))  16.2 us
    ppermute x14, starting transfers between devices, run(): got.append(lax.ppermute(packs[2 * axis + odd], ('gx', 'gy'), pairs))  15.2 us
    all_to_all x1, blocking collectives, body(): sums = lax.all_to_all(sums, ('gx', 'gy'), 0, 0, tiled=True)  13.5 us
    pallas_call x7, Pallas kernels, call(): pl.pallas_call(kernel, name='level', in_specs=[SSPEC] + [VSPEC] * 4 + [pl...  4.62 us
    pallas_call x1, Pallas kernels, call(): pl.pallas_call(kernel, name='prepare', in_specs=[pl.BlockSpec(memory_spac...  2.94 us
    ppermute x1, starting transfers between devices, body(): color_y = lax.ppermute(coloring, 'gy', [(j, j ^ 1) for j in range(plan.ny)])  2.64 us
    pallas_call x1, Pallas kernels, call(): pl.pallas_call(kernel, name='begin', in_specs=[SSPEC] + [pl.BlockSpec(mem...  2.06 us
  transfers between devices with their start and end apart: 16, of which 10 were waited for; matrix products, arithmetic and copies ran while one was open for 0% of the time, Pallas kernels for 5%

commit v1 on v0

--- a/solution.py
+++ b/solution.py
@@ -108,9 +108,7 @@
     return high, low
 
 
-def update(plan, second, state, coupling, inverse, kept, rest, source, result, sem):
-    again = piece_copy(plan, CHUNKS, inverse, kept, rest, sem)
-    again.start()
+def update(plan, second, state, coupling, kept, rest, source, result):
     pad = plan.pad
     values = jnp.concatenate([state[n * pad:(n + 1) * pad, :] for n in range(3)], axis=1)
     high, low = parts_of(values)
@@ -122,7 +120,6 @@
     source[...] = (right + couple).astype(jnp.bfloat16).astype(jnp.float32)
     result[pad - SUB:pad, :] = jnp.zeros((SUB, LANES), jnp.float32)
     apply_inverse(plan, kept, source, result, 0, 0, plan.held)
-    again.wait()
     apply_inverse(plan, rest, source, result, plan.held, 0, plan.rows - plan.held)
     finish(plan, second, state, result)
 
@@ -299,8 +296,30 @@
     return call
 
 
+def fetch_kernel(plan, name, receives):
+    def kernel(inverse, rest, sem):
+        @pl.when(receives(lax.axis_index("gx") & 1, lax.axis_index("gy") & 1))
+        def _():
+            copy = piece_copy(plan, CHUNKS, inverse, None, rest, sem)
+            copy.start()
+            copy.wait()
+
+    def call(inverse):
+        return pl.pallas_call(
+            kernel,
+            name=name,
+            in_specs=[pl.BlockSpec(memory_space=pltpu.HBM)],
+            out_specs=VSPEC,
+            out_shape=plan.rest_type(inverse),
+            compiler_params=pltpu.CompilerParams(vmem_limit_bytes=VMEM_LIMIT),
+            scratch_shapes=[pltpu.SemaphoreType.DMA],
+        )(hbm(inverse))
+
+    return call
+
+
 def level_kernel(plan):
-    def kernel(control, old_state, coupling, table, kept, inverse, state, xe, xo, ye, yo, rest, source, result, sem):
+    def kernel(control, old_state, coupling, table, kept, rest, state, xe, xo, ye, yo, source, result):
         del old_state
         steps = state[plan.step:plan.step + SUB, :] + 1.0
         state[plan.step:plan.step + SUB, :] = steps
@@ -310,27 +329,25 @@
 
         @pl.when(turn)
         def _():
-            update(plan, second, state, coupling, inverse, kept, rest, source, result, sem)
+            update(plan, second, state, coupling, kept, rest, source, result)
 
         for n, ref in enumerate((xe, xo, ye, yo)):
             write_pack(plan, state, table, n, ref)
 
-    def call(control, state, coupling, table, kept, inverse):
+    def call(control, state, coupling, table, kept, rest):
         return pl.pallas_call(
             kernel,
             name="level",
-            in_specs=[SSPEC] + [VSPEC] * 4 + [pl.BlockSpec(memory_space=pltpu.HBM)],
+            in_specs=[SSPEC] + [VSPEC] * 5,
             out_specs=[VSPEC] * 5,
             out_shape=[plan.state_type] + [plan.pack_type] * 4,
             input_output_aliases={1: 0},
             compiler_params=pltpu.CompilerParams(vmem_limit_bytes=VMEM_LIMIT),
             scratch_shapes=[
-                plan.rest_type(inverse),
                 pltpu.VMEM((plan.pad, LANES), jnp.float32),
                 pltpu.VMEM((plan.pad, LANES), jnp.float32),
-                pltpu.SemaphoreType.DMA,
             ],
-        )(smem(control), *(vmem(v) for v in (state, coupling, table, kept)), hbm(inverse))
+        )(smem(control), *(vmem(v) for v in (state, coupling, table, kept, rest)))
 
     return call
 
@@ -401,7 +418,7 @@
     def receives(i, j):
         return ((i if axes == (0,) else j if axes == (1,) else i ^ j) & 1) != parity
 
-    def run(state, *packs):
+    def run(inverse, control, kept, coupling, table, state, *packs):
         got = []
         for n, (axis, odd) in enumerate(steps):
             if len(axes) == 1 and odd:
@@ -409,7 +426,9 @@
             else:
                 pairs = edge_pairs(plan, axis, odd, sends, n == len(steps) - 1)
             got.append(lax.ppermute(packs[2 * axis + odd], ("gx", "gy"), pairs))
-        return merge_kernel(plan, name, receives, steps)(state, got)
+        rest = fetch_kernel(plan, f"fetch_{name}", receives)(inverse)
+        state = merge_kernel(plan, name, receives, steps)(state, got)
+        return tuple(level_kernel(plan)(control, state, coupling, table, kept, rest))
 
     return run
 
@@ -431,8 +450,8 @@
 
         def turn(carry):
             code, state, packs = carry
-            state = lax.switch((code & 7) - 1, flows, state, *packs)
-            state, *packs = level_kernel(plan)(control, state, coupling, table, kept, inverse[0])
+            state, *packs = lax.switch(
+                (code & 7) - 1, flows, inverse[0], control, kept, coupling, table, state, *packs)
             return code >> 4, state, tuple(packs)
 
         state = lax.while_loop(lambda carry: carry[0] != 0, turn, (code[0], state, tuple(packs)))[1]

time: 60.8 us -> 59.3 us (0.975)
  waiting for transfers between devices: 16.2 us -> 10.8 us
  Pallas kernels: 10.6 us -> 13.5 us
  starting transfers between devices: 18.4 us -> 20.9 us
  blocking collectives: 13.5 us -> 11.7 us
    ppermute x14, waiting for transfers between devices: 16.2 us -> 10.8 us  [run(): got.append(lax.ppermute(packs[2 * axis + odd], ('gx', 'gy'), pairs))]
    pallas_call x7 -> x14, Pallas kernels: 4.62 us -> 7.51 us  [the longest x7 3.84 us: call(): pl.pallas_call(kernel, name=name, in_specs=[pl.BlockSpec(memory_space=plt...]
    ppermute x14, starting transfers between devices: 15.2 us -> 17.7 us  [run(): got.append(lax.ppermute(packs[2 * axis + odd], ('gx', 'gy'), pairs))]
    all_to_all x1, blocking collectives: 13.5 us -> 11.7 us  [body(): sums = lax.all_to_all(sums, ('gx', 'gy'), 0, 0, tiled=True)]
  transfers between devices with their start and end apart: 16 -> 16, of which waited for: 10 -> 7; matrix products, arithmetic and copies ran while one was open for 0% -> 0% of each run, Pallas kernels for 5% -> 11%
where the time goes in v1:
time: 59.3 us; the launch traced here: 59.7 us
  starting transfers between devices  20.9 us (35%)
  Pallas kernels  13.5 us (23%)
  blocking collectives  11.7 us (20%)
  waiting for transfers between devices  10.8 us (18%)
  between operations  1.36 us (2%)
  loops' own time  0.95 us (2%)
    ppermute x14, starting transfers between devices, run(): got.append(lax.ppermute(packs[2 * axis + odd], ('gx', 'gy'), pairs))  17.7 us
    all_to_all x1, blocking collectives, body(): sums = lax.all_to_all(sums, ('gx', 'gy'), 0, 0, tiled=True)  11.7 us
    ppermute x14, waiting for transfers between devices, run(): got.append(lax.ppermute(packs[2 * axis + odd], ('gx', 'gy'), pairs))  10.8 us
    pallas_call x7, Pallas kernels, call(): pl.pallas_call(kernel, name=name, in_specs=[pl.BlockSpec(memory_space=plt...  3.84 us
    pallas_call x7, Pallas kernels, call(): pl.pallas_call(kernel, name='level', in_specs=[SSPEC] + [VSPEC] * 5, out_...  3.67 us
    pallas_call x1, Pallas kernels, call(): pl.pallas_call(kernel, name='prepare', in_specs=[pl.BlockSpec(memory_spac...  2.94 us
    ppermute x1, starting transfers between devices, body(): color_y = lax.ppermute(coloring, 'gy', [(j, j ^ 1) for j in range(plan.ny)])  2.64 us
    pallas_call x1, Pallas kernels, call(): pl.pallas_call(kernel, name='begin', in_specs=[SSPEC] + [pl.BlockSpec(mem...  2.1 us
  transfers between devices with their start and end apart: 16, of which 7 were waited for; matrix products, arithmetic and copies ran while one was open for 0% of the time, Pallas kernels for 11%

profile of v1, /device:TPU:0, one launch (start us, length us, event | category | flops | bytes accessed | tf_op | source)
XLA Modules:
  0.0 59.7 jit_solution(8374909964618540964)
XLA Ops:
  1.2 2.6 %collective-permute-start.17 = (s32[1,1]{1,0:T(1,128)}, s32[1,1]{1,0:T(1,128)}, u32[]{:S(2)}, u32[]{:S(2)}) collective-permute-start(s32[1,1]{1,0:T(1,128)} %param.19), channel_id=1, source_target_pairs={{0,1},{1,0},{2,3},{3,2},{4,5},{5,4},{6,7},{7,6},{8,9},{9,8},{10,11... | collective-permute-start | bytes 20 | tf_op jit(solution)/shard_map/ppermute | solution.py:441
  4.5 2.9 %prepare.1 = (bf16[90,125,128]{2,1,0:T(8,128)(2,1)S(1)}, f32[536,128]{1,0:T(8,128)S(1)}, bf16[768,128]{1,0:T(8,128)(2,1)S(1)}, s32[8,128]{1,0:T(8,128)S(1)}) custom-call(f32[125,1,128]{2,1,0:T(1,128)} %bitcast.23, f32[4,128]{1,0:T(4,128)} %bitcast.24, s32[4,128]{1,0:T(4,128)} %bitcast.25, s32[4,64]{1,0:T(4,128)} %bitcast.26, bf16[125,125,128]{2,1,0:T(8,128)(2,1)} %bitcast.15), custom_call_target="tpu_custom_call" | custom-call | tf_op jit(solution)/shard_map/prepare/pallas_call | solution.py:184
  7.5 2.1 %begin.1 = (s32[1]{0:T(128)S(4)}, s32[2]{0:T(128)S(4)}, f32[536,128]{1,0:T(8,128)S(1)}, f32[64,128]{1,0:T(8,128)S(1)}, f32[64,128]{1,0:T(8,128)S(1)}, /*index=5*/f32[64,128]{1,0:T(8,128)S(1)}, f32[64,128]{1,0:T(8,128)S(1)}) custom-call(s32[1,1]{1,0:T(1,128)S(6)} %copy.83.color, ...), custom_call_target="tpu_custom_call", output_to_operand_aliasing={{2}: (3, {})} | custom-call | tf_op jit(solution)/shard_map/begin/pallas_call | solution.py:253
  9.6 37.2 %while.20 = (s32[]{:T(128)S(4)}, f32[536,128]{1,0:T(8,128)S(1)}, f32[64,128]{1,0:T(8,128)S(1)}, f32[64,128]{1,0:T(8,128)S(1)}, f32[64,128]{1,0:T(8,128)S(1)}, /*...) while((s32[]{:T(128)S(4)}, f32[536,128]{1,0:T(8,128)S(1)}, ...), condition=%wide.region_7.0_spmd, body=%wide.region_0.0_spmd.sunk | while | flops 5 | bytes 525061 | solution.py:457
  9.6 6.6 %conditional.2 = ((f32[536,128]{1,0:T(8,128)S(1)}, f32[64,128]{1,0:T(8,128)S(1)}, f32[64,128]{1,0:T(8,128)S(1)}, f32[64,128]{1,0:T(8,128)S(1)}, f32[64,128]{1,0:T(8,128)S(1)})) conditional(s32[]{:T(128)} %clamp.7, (f32[64,128]{1,0:T(8,128)S(1)}, f32[64,128]{1,0:T(8,128)S(1)}, f32[536,128]{1,0:T(8,128)S(1)}, ...), branch_computations={%region_1.0_spmd, %region_2.0_spmd, %region_3.0_spmd, %region_4.0_... | conditional | bytes 524456 | solution.py:453
  9.8 3.0 %collective-permute-start.7 = (f32[64,128]{1,0:T(8,128)S(1)}, f32[64,128]{1,0:T(8,128)S(1)}, u32[]{:S(2)}, u32[]{:S(2)}) collective-permute-start(f32[64,128]{1,0:T(8,128)S(1)} %get-tuple-element.265), channel_id=1, source_target_pairs={{0,1},{1,0},{2,3},{3,2},{4,5},{5,4},{6,7},{7,6},{8,9},{9,8},{10,11... | collective-permute-start | bytes 98312 | tf_op jit(solution)/shard_map/while/body/cond/branch_3_fun/ppermute | solution.py:428
  12.8 1.3 %fetch_along_y1.1.rest = bf16[35,125,128]{2,1,0:T(8,128)(2,1)S(1)} custom-call(bf16[125,125,128]{2,1,0:T(8,128)(2,1)} %get-tuple-element.269.inverse), custom_call_target="tpu_custom_call" | custom-call | tf_op jit(solution)/shard_map/while/body/cond/branch_3_fun/fetch_along_y1/pallas_call | solution.py:308
  14.8 1.4 %level.9 = (f32[536,128]{1,0:T(8,128)S(1)}, f32[64,128]{1,0:T(8,128)S(1)}, f32[64,128]{1,0:T(8,128)S(1)}, f32[64,128]{1,0:T(8,128)S(1)}, f32[64,128]{1,0:T(8,128)S(1)}) custom-call(s32[2]{0:T(128)S(4)} %get-tuple-element.262.control, f32[536,128]{1,0:T(8,128)S(1)} %along_y1.1.old_state, ...), custom_call_target="tpu_custom_call", output_to_operand_aliasing={{0}: (1, {})} | custom-call | tf_op jit(solution)/shard_map/while/body/cond/branch_3_fun/level/pallas_call | solution.py:338
  16.3 4.2 %conditional.2 = ((f32[536,128]{1,0:T(8,128)S(1)}, f32[64,128]{1,0:T(8,128)S(1)}, f32[64,128]{1,0:T(8,128)S(1)}, f32[64,128]{1,0:T(8,128)S(1)}, f32[64,128]{1,0:T(8,128)S(1)})) conditional(s32[]{:T(128)} %clamp.7, (f32[64,128]{1,0:T(8,128)S(1)}, f32[64,128]{1,0:T(8,128)S(1)}, f32[536,128]{1,0:T(8,128)S(1)}, ...), branch_computations={%region_1.0_spmd, %region_2.0_spmd, %region_3.0_spmd, %region_4.0_... | conditional | bytes 524456 | solution.py:453
  16.3 0.8 %collective-permute-start = (f32[64,128]{1,0:T(8,128)S(1)}, f32[64,128]{1,0:T(8,128)S(1)}, u32[]{:S(2)}, u32[]{:S(2)}) collective-permute-start(f32[64,128]{1,0:T(8,128)S(1)} %get-tuple-element.240), channel_id=1, source_target_pairs={{0,1},{1,0},{2,3},{3,2},{4,9},{5,8},{6,11},{7,10},{8,4},{9,5},{10,... | collective-permute-start | bytes 98312 | tf_op jit(solution)/shard_map/while/body/cond/branch_0_fun/ppermute | solution.py:428
  17.1 1.0 %collective-permute-start.1 = (f32[64,128]{1,0:T(8,128)S(1)}, f32[64,128]{1,0:T(8,128)S(1)}, u32[]{:S(2)}, u32[]{:S(2)}) collective-permute-start(f32[64,128]{1,0:T(8,128)S(1)} %get-tuple-element.241), channel_id=1, source_target_pairs={{0,4},{1,5},{2,6},{3,7},{4,0},{5,1},{6,2},{7,3},{8,12},{9,13},{10,... | collective-permute-start | bytes 98312 | tf_op jit(solution)/shard_map/while/body/cond/branch_0_fun/ppermute | solution.py:428
  18.2 2.1 %collective-permute-done.refs_1_ = f32[64,128]{1,0:T(8,128)S(1)} collective-permute-done((f32[64,128]{1,0:T(8,128)S(1)}, f32[64,128]{1,0:T(8,128)S(1)}, u32[]{:S(2)}, u32[]{:S(2)}) %collective-permute-start) | collective-permute-done | bytes 32800 | tf_op jit(solution)/shard_map/while/body/cond/branch_0_fun/ppermute | solution.py:428
  20.6 4.8 %conditional.2 = ((f32[536,128]{1,0:T(8,128)S(1)}, f32[64,128]{1,0:T(8,128)S(1)}, f32[64,128]{1,0:T(8,128)S(1)}, f32[64,128]{1,0:T(8,128)S(1)}, f32[64,128]{1,0:T(8,128)S(1)})) conditional(s32[]{:T(128)} %clamp.7, (f32[64,128]{1,0:T(8,128)S(1)}, f32[64,128]{1,0:T(8,128)S(1)}, f32[536,128]{1,0:T(8,128)S(1)}, ...), branch_computations={%region_1.0_spmd, %region_2.0_spmd, %region_3.0_spmd, %region_4.0_... | conditional | bytes 524456 | solution.py:453
  21.2 1.7 %collective-permute-start.3 = (f32[64,128]{1,0:T(8,128)S(1)}, f32[64,128]{1,0:T(8,128)S(1)}, u32[]{:S(2)}, u32[]{:S(2)}) collective-permute-start(f32[64,128]{1,0:T(8,128)S(1)} %get-tuple-element.249), channel_id=1, source_target_pairs={{0,1},{1,0},{2,3},{3,2},{4,5},{5,4},{6,7},{7,6},{8,9},{9,8},{10,11... | collective-permute-start | bytes 98312 | tf_op jit(solution)/shard_map/while/body/cond/branch_1_fun/ppermute | solution.py:428
  22.9 2.2 %collective-permute-done.3.refs_2_ = f32[64,128]{1,0:T(8,128)S(1)} collective-permute-done((f32[64,128]{1,0:T(8,128)S(1)}, f32[64,128]{1,0:T(8,128)S(1)}, u32[]{:S(2)}, u32[]{:S(2)}) %collective-permute-start.3) | collective-permute-done | bytes 32800 | tf_op jit(solution)/shard_map/while/body/cond/branch_1_fun/ppermute | solution.py:428
  25.4 4.3 %conditional.2 = ((f32[536,128]{1,0:T(8,128)S(1)}, f32[64,128]{1,0:T(8,128)S(1)}, f32[64,128]{1,0:T(8,128)S(1)}, f32[64,128]{1,0:T(8,128)S(1)}, f32[64,128]{1,0:T(8,128)S(1)})) conditional(s32[]{:T(128)} %clamp.7, (f32[64,128]{1,0:T(8,128)S(1)}, f32[64,128]{1,0:T(8,128)S(1)}, f32[536,128]{1,0:T(8,128)S(1)}, ...), branch_computations={%region_1.0_spmd, %region_2.0_spmd, %region_3.0_spmd, %region_4.0_... | conditional | bytes 524456 | solution.py:453
  25.4 1.9 %collective-permute-start.4 = (f32[64,128]{1,0:T(8,128)S(1)}, f32[64,128]{1,0:T(8,128)S(1)}, u32[]{:S(2)}, u32[]{:S(2)}) collective-permute-start(f32[64,128]{1,0:T(8,128)S(1)} %get-tuple-element.256), channel_id=1, source_target_pairs={{0,1},{1,0},{2,3},{3,2},{4,8},{5,9},{6,10},{7,11},{8,5},{9,4},{10,... | collective-permute-start | bytes 98312 | tf_op jit(solution)/shard_map/while/body/cond/branch_2_fun/ppermute | solution.py:428
  27.3 1.3 %fetch_along_x1.1.rest = bf16[35,125,128]{2,1,0:T(8,128)(2,1)S(1)} custom-call(bf16[125,125,128]{2,1,0:T(8,128)(2,1)} %get-tuple-element.261.inverse), custom_call_target="tpu_custom_call" | custom-call | tf_op jit(solution)/shard_map/while/body/cond/branch_2_fun/fetch_along_x1/pallas_call | solution.py:308
  28.6 0.8 %collective-permute-done.4.refs_1_ = f32[64,128]{1,0:T(8,128)S(1)} collective-permute-done((f32[64,128]{1,0:T(8,128)S(1)}, f32[64,128]{1,0:T(8,128)S(1)}, u32[]{:S(2)}, u32[]{:S(2)}) %collective-permute-start.4) | collective-permute-done | bytes 32800 | tf_op jit(solution)/shard_map/while/body/cond/branch_2_fun/ppermute | solution.py:428
  29.8 6.5 %conditional.2 = ((f32[536,128]{1,0:T(8,128)S(1)}, f32[64,128]{1,0:T(8,128)S(1)}, f32[64,128]{1,0:T(8,128)S(1)}, f32[64,128]{1,0:T(8,128)S(1)}, f32[64,128]{1,0:T(8,128)S(1)})) conditional(s32[]{:T(128)} %clamp.7, (f32[64,128]{1,0:T(8,128)S(1)}, f32[64,128]{1,0:T(8,128)S(1)}, f32[536,128]{1,0:T(8,128)S(1)}, ...), branch_computations={%region_1.0_spmd, %region_2.0_spmd, %region_3.0_spmd, %region_4.0_... | conditional | bytes 524456 | solution.py:453
  30.3 2.6 %collective-permute-start.7 = (f32[64,128]{1,0:T(8,128)S(1)}, f32[64,128]{1,0:T(8,128)S(1)}, u32[]{:S(2)}, u32[]{:S(2)}) collective-permute-start(f32[64,128]{1,0:T(8,128)S(1)} %get-tuple-element.265), channel_id=1, source_target_pairs={{0,1},{1,0},{2,3},{3,2},{4,5},{5,4},{6,7},{7,6},{8,9},{9,8},{10,11... | collective-permute-start | bytes 98312 | tf_op jit(solution)/shard_map/while/body/cond/branch_3_fun/ppermute | solution.py:428
  32.9 1.3 %fetch_along_y1.1.rest = bf16[35,125,128]{2,1,0:T(8,128)(2,1)S(1)} custom-call(bf16[125,125,128]{2,1,0:T(8,128)(2,1)} %get-tuple-element.269.inverse), custom_call_target="tpu_custom_call" | custom-call | tf_op jit(solution)/shard_map/while/body/cond/branch_3_fun/fetch_along_y1/pallas_call | solution.py:308
  34.9 1.4 %level.9 = (f32[536,128]{1,0:T(8,128)S(1)}, f32[64,128]{1,0:T(8,128)S(1)}, f32[64,128]{1,0:T(8,128)S(1)}, f32[64,128]{1,0:T(8,128)S(1)}, f32[64,128]{1,0:T(8,128)S(1)}) custom-call(s32[2]{0:T(128)S(4)} %get-tuple-element.262.control, f32[536,128]{1,0:T(8,128)S(1)} %along_y1.1.old_state, ...), custom_call_target="tpu_custom_call", output_to_operand_aliasing={{0}: (1, {})} | custom-call | tf_op jit(solution)/shard_map/while/body/cond/branch_3_fun/level/pallas_call | solution.py:338
  36.3 4.3 %conditional.2 = ((f32[536,128]{1,0:T(8,128)S(1)}, f32[64,128]{1,0:T(8,128)S(1)}, f32[64,128]{1,0:T(8,128)S(1)}, f32[64,128]{1,0:T(8,128)S(1)}, f32[64,128]{1,0:T(8,128)S(1)})) conditional(s32[]{:T(128)} %clamp.7, (f32[64,128]{1,0:T(8,128)S(1)}, f32[64,128]{1,0:T(8,128)S(1)}, f32[536,128]{1,0:T(8,128)S(1)}, ...), branch_computations={%region_1.0_spmd, %region_2.0_spmd, %region_3.0_spmd, %region_4.0_... | conditional | bytes 524456 | solution.py:453
  36.4 0.8 %collective-permute-start = (f32[64,128]{1,0:T(8,128)S(1)}, f32[64,128]{1,0:T(8,128)S(1)}, u32[]{:S(2)}, u32[]{:S(2)}) collective-permute-start(f32[64,128]{1,0:T(8,128)S(1)} %get-tuple-element.240), channel_id=1, source_target_pairs={{0,1},{1,0},{2,3},{3,2},{4,9},{5,8},{6,11},{7,10},{8,4},{9,5},{10,... | collective-permute-start | bytes 98312 | tf_op jit(solution)/shard_map/while/body/cond/branch_0_fun/ppermute | solution.py:428
  37.2 0.7 %collective-permute-start.1 = (f32[64,128]{1,0:T(8,128)S(1)}, f32[64,128]{1,0:T(8,128)S(1)}, u32[]{:S(2)}, u32[]{:S(2)}) collective-permute-start(f32[64,128]{1,0:T(8,128)S(1)} %get-tuple-element.241), channel_id=1, source_target_pairs={{0,4},{1,5},{2,6},{3,7},{4,0},{5,1},{6,2},{7,3},{8,12},{9,13},{10,... | collective-permute-start | bytes 98312 | tf_op jit(solution)/shard_map/while/body/cond/branch_0_fun/ppermute | solution.py:428
  37.8 2.6 %collective-permute-done.refs_1_ = f32[64,128]{1,0:T(8,128)S(1)} collective-permute-done((f32[64,128]{1,0:T(8,128)S(1)}, f32[64,128]{1,0:T(8,128)S(1)}, u32[]{:S(2)}, u32[]{:S(2)}) %collective-permute-start) | collective-permute-done | bytes 32800 | tf_op jit(solution)/shard_map/while/body/cond/branch_0_fun/ppermute | solution.py:428
  40.7 6.1 %conditional.2 = ((f32[536,128]{1,0:T(8,128)S(1)}, f32[64,128]{1,0:T(8,128)S(1)}, f32[64,128]{1,0:T(8,128)S(1)}, f32[64,128]{1,0:T(8,128)S(1)}, f32[64,128]{1,0:T(8,128)S(1)})) conditional(s32[]{:T(128)} %clamp.7, (f32[64,128]{1,0:T(8,128)S(1)}, f32[64,128]{1,0:T(8,128)S(1)}, f32[536,128]{1,0:T(8,128)S(1)}, ...), branch_computations={%region_1.0_spmd, %region_2.0_spmd, %region_3.0_spmd, %region_4.0_... | conditional | bytes 524456 | solution.py:453
  41.1 3.5 %collective-permute-start.3 = (f32[64,128]{1,0:T(8,128)S(1)}, f32[64,128]{1,0:T(8,128)S(1)}, u32[]{:S(2)}, u32[]{:S(2)}) collective-permute-start(f32[64,128]{1,0:T(8,128)S(1)} %get-tuple-element.249), channel_id=1, source_target_pairs={{0,1},{1,0},{2,3},{3,2},{4,5},{5,4},{6,7},{7,6},{8,9},{9,8},{10,11... | collective-permute-start | bytes 98312 | tf_op jit(solution)/shard_map/while/body/cond/branch_1_fun/ppermute | solution.py:428
  44.7 1.9 %collective-permute-done.3.refs_2_ = f32[64,128]{1,0:T(8,128)S(1)} collective-permute-done((f32[64,128]{1,0:T(8,128)S(1)}, f32[64,128]{1,0:T(8,128)S(1)}, u32[]{:S(2)}, u32[]{:S(2)}) %collective-permute-start.3) | collective-permute-done | bytes 32800 | tf_op jit(solution)/shard_map/while/body/cond/branch_1_fun/ppermute | solution.py:428
  46.8 0.7 %last.1 = (f32[125,1,128]{2,1,0:T(1,128)}, f32[32,128]{1,0:T(8,128)S(1)}) custom-call(f32[536,128]{1,0:T(8,128)S(1)} %get-tuple-element.334.state), custom_call_target="tpu_custom_call" | custom-call | tf_op jit(solution)/shard_map/last/pallas_call | solution.py:366
  47.5 11.7 %all_to_all.12 = f32[32,1,128]{2,1,0:T(1,128)S(1)} all-to-all(f32[32,1,128]{2,1,0:T(1,128)S(1)} %bitcast.14), channel_id=1, replica_groups=mesh['gx'=8,'gy'=4] {'gx','gy'}, dimensions={0} | all-to-all | bytes 32768 | tf_op jit(solution)/shard_map/all_to_all | solution.py:459
  (35 shorter events, 5.2 us)
Async XLA Ops:
  0.6 6.8 %collective-permute-start.16 = (s32[1,1]{1,0:T(1,128)}, s32[1,1]{1,0:T(1,128)}, u32[]{:S(2)}, u32[]{:S(2)}) collective-permute-start(s32[1,1]{1,0:T(1,128)} %param.19), channel_id=1, source_target_pairs={{0,4},{4,0},{8,12},{12,8},{16,20},{20,16},{24,28},{28,24},{1,5},{5... | collective-permute-start | bytes 20 | tf_op jit(solution)/shard_map/ppermute | solution.py:440
  1.2 6.3 %collective-permute-start.17 = (s32[1,1]{1,0:T(1,128)}, s32[1,1]{1,0:T(1,128)}, u32[]{:S(2)}, u32[]{:S(2)}) collective-permute-start(s32[1,1]{1,0:T(1,128)} %param.19), channel_id=1, source_target_pairs={{0,1},{1,0},{2,3},{3,2},{4,5},{5,4},{6,7},{7,6},{8,9},{9,8},{10,11... | collective-permute-start | bytes 20 | tf_op jit(solution)/shard_map/ppermute | solution.py:441
  9.6 4.5 %collective-permute-start.6 = (f32[64,128]{1,0:T(8,128)S(1)}, f32[64,128]{1,0:T(8,128)S(1)}, u32[]{:S(2)}, u32[]{:S(2)}) collective-permute-start(f32[64,128]{1,0:T(8,128)S(1)} %get-tuple-element.264), channel_id=1, source_target_pairs={{0,4},{1,2},{2,5},{3,7},{4,0},{5,6},{6,1},{7,3},{8,12},{9,10},{10,... | collective-permute-start | bytes 98312 | tf_op jit(solution)/shard_map/while/body/cond/branch_3_fun/ppermute | solution.py:428
  9.8 4.9 %collective-permute-start.7 = (f32[64,128]{1,0:T(8,128)S(1)}, f32[64,128]{1,0:T(8,128)S(1)}, u32[]{:S(2)}, u32[]{:S(2)}) collective-permute-start(f32[64,128]{1,0:T(8,128)S(1)} %get-tuple-element.265), channel_id=1, source_target_pairs={{0,1},{1,0},{2,3},{3,2},{4,5},{5,4},{6,7},{7,6},{8,9},{9,8},{10,11... | collective-permute-start | bytes 98312 | tf_op jit(solution)/shard_map/while/body/cond/branch_3_fun/ppermute | solution.py:428
  16.3 4.0 %collective-permute-start = (f32[64,128]{1,0:T(8,128)S(1)}, f32[64,128]{1,0:T(8,128)S(1)}, u32[]{:S(2)}, u32[]{:S(2)}) collective-permute-start(f32[64,128]{1,0:T(8,128)S(1)} %get-tuple-element.240), channel_id=1, source_target_pairs={{0,1},{1,0},{2,3},{3,2},{4,9},{5,8},{6,11},{7,10},{8,4},{9,5},{10,... | collective-permute-start | bytes 98312 | tf_op jit(solution)/shard_map/while/body/cond/branch_0_fun/ppermute | solution.py:428
  17.1 3.2 %collective-permute-start.1 = (f32[64,128]{1,0:T(8,128)S(1)}, f32[64,128]{1,0:T(8,128)S(1)}, u32[]{:S(2)}, u32[]{:S(2)}) collective-permute-start(f32[64,128]{1,0:T(8,128)S(1)} %get-tuple-element.241), channel_id=1, source_target_pairs={{0,4},{1,5},{2,6},{3,7},{4,0},{5,1},{6,2},{7,3},{8,12},{9,13},{10,... | collective-permute-start | bytes 98312 | tf_op jit(solution)/shard_map/while/body/cond/branch_0_fun/ppermute | solution.py:428
  20.6 2.3 %collective-permute-start.2 = (f32[64,128]{1,0:T(8,128)S(1)}, f32[64,128]{1,0:T(8,128)S(1)}, u32[]{:S(2)}, u32[]{:S(2)}) collective-permute-start(f32[64,128]{1,0:T(8,128)S(1)} %get-tuple-element.248), channel_id=1, source_target_pairs={{0,4},{1,6},{2,1},{3,7},{4,0},{5,2},{6,5},{7,3},{8,12},{9,14},{10,... | collective-permute-start | bytes 98312 | tf_op jit(solution)/shard_map/while/body/cond/branch_1_fun/ppermute | solution.py:428
  21.2 3.9 %collective-permute-start.3 = (f32[64,128]{1,0:T(8,128)S(1)}, f32[64,128]{1,0:T(8,128)S(1)}, u32[]{:S(2)}, u32[]{:S(2)}) collective-permute-start(f32[64,128]{1,0:T(8,128)S(1)} %get-tuple-element.249), channel_id=1, source_target_pairs={{0,1},{1,0},{2,3},{3,2},{4,5},{5,4},{6,7},{7,6},{8,9},{9,8},{10,11... | collective-permute-start | bytes 98312 | tf_op jit(solution)/shard_map/while/body/cond/branch_1_fun/ppermute | solution.py:428
  25.4 4.0 %collective-permute-start.4 = (f32[64,128]{1,0:T(8,128)S(1)}, f32[64,128]{1,0:T(8,128)S(1)}, u32[]{:S(2)}, u32[]{:S(2)}) collective-permute-start(f32[64,128]{1,0:T(8,128)S(1)} %get-tuple-element.256), channel_id=1, source_target_pairs={{0,1},{1,0},{2,3},{3,2},{4,8},{5,9},{6,10},{7,11},{8,5},{9,4},{10,... | collective-permute-start | bytes 98312 | tf_op jit(solution)/shard_map/while/body/cond/branch_2_fun/ppermute | solution.py:428
  27.3 2.1 %collective-permute-start.5 = (f32[64,128]{1,0:T(8,128)S(1)}, f32[64,128]{1,0:T(8,128)S(1)}, u32[]{:S(2)}, u32[]{:S(2)}) collective-permute-start(f32[64,128]{1,0:T(8,128)S(1)} %get-tuple-element.257), channel_id=1, source_target_pairs={{0,4},{1,5},{2,6},{3,7},{4,0},{5,1},{6,2},{7,3},{8,12},{9,13},{10,... | collective-permute-start | bytes 98312 | tf_op jit(solution)/shard_map/while/body/cond/branch_2_fun/ppermute | solution.py:428
  29.8 4.4 %collective-permute-start.6 = (f32[64,128]{1,0:T(8,128)S(1)}, f32[64,128]{1,0:T(8,128)S(1)}, u32[]{:S(2)}, u32[]{:S(2)}) collective-permute-start(f32[64,128]{1,0:T(8,128)S(1)} %get-tuple-element.264), channel_id=1, source_target_pairs={{0,4},{1,2},{2,5},{3,7},{4,0},{5,6},{6,1},{7,3},{8,12},{9,10},{10,... | collective-permute-start | bytes 98312 | tf_op jit(solution)/shard_map/while/body/cond/branch_3_fun/ppermute | solution.py:428
  30.3 4.5 %collective-permute-start.7 = (f32[64,128]{1,0:T(8,128)S(1)}, f32[64,128]{1,0:T(8,128)S(1)}, u32[]{:S(2)}, u32[]{:S(2)}) collective-permute-start(f32[64,128]{1,0:T(8,128)S(1)} %get-tuple-element.265), channel_id=1, source_target_pairs={{0,1},{1,0},{2,3},{3,2},{4,5},{5,4},{6,7},{7,6},{8,9},{9,8},{10,11... | collective-permute-start | bytes 98312 | tf_op jit(solution)/shard_map/while/body/cond/branch_3_fun/ppermute | solution.py:428
  36.4 4.1 %collective-permute-start = (f32[64,128]{1,0:T(8,128)S(1)}, f32[64,128]{1,0:T(8,128)S(1)}, u32[]{:S(2)}, u32[]{:S(2)}) collective-permute-start(f32[64,128]{1,0:T(8,128)S(1)} %get-tuple-element.240), channel_id=1, source_target_pairs={{0,1},{1,0},{2,3},{3,2},{4,9},{5,8},{6,11},{7,10},{8,4},{9,5},{10,... | collective-permute-start | bytes 98312 | tf_op jit(solution)/shard_map/while/body/cond/branch_0_fun/ppermute | solution.py:428
  37.2 3.3 %collective-permute-start.1 = (f32[64,128]{1,0:T(8,128)S(1)}, f32[64,128]{1,0:T(8,128)S(1)}, u32[]{:S(2)}, u32[]{:S(2)}) collective-permute-start(f32[64,128]{1,0:T(8,128)S(1)} %get-tuple-element.241), channel_id=1, source_target_pairs={{0,4},{1,5},{2,6},{3,7},{4,0},{5,1},{6,2},{7,3},{8,12},{9,13},{10,... | collective-permute-start | bytes 98312 | tf_op jit(solution)/shard_map/while/body/cond/branch_0_fun/ppermute | solution.py:428
  40.8 4.0 %collective-permute-start.2 = (f32[64,128]{1,0:T(8,128)S(1)}, f32[64,128]{1,0:T(8,128)S(1)}, u32[]{:S(2)}, u32[]{:S(2)}) collective-permute-start(f32[64,128]{1,0:T(8,128)S(1)} %get-tuple-element.248), channel_id=1, source_target_pairs={{0,4},{1,6},{2,1},{3,7},{4,0},{5,2},{6,5},{7,3},{8,12},{9,14},{10,... | collective-permute-start | bytes 98312 | tf_op jit(solution)/shard_map/while/body/cond/branch_1_fun/ppermute | solution.py:428
  41.1 5.4 %collective-permute-start.3 = (f32[64,128]{1,0:T(8,128)S(1)}, f32[64,128]{1,0:T(8,128)S(1)}, u32[]{:S(2)}, u32[]{:S(2)}) collective-permute-start(f32[64,128]{1,0:T(8,128)S(1)} %get-tuple-element.249), channel_id=1, source_target_pairs={{0,1},{1,0},{2,3},{3,2},{4,5},{5,4},{6,7},{7,6},{8,9},{9,8},{10,11... | collective-permute-start | bytes 98312 | tf_op jit(solution)/shard_map/while/body/cond/branch_1_fun/ppermute | solution.py:428
